TPU v7x, 256 devices: a whole 4x4x8 slice. The times are simulated.
256 devices in a mesh: span: 256 (over y, x, z, core).
Axes of the slice: x: 4, y: 4, z: 8, core: 2. Of those that a mesh axis runs over, the one named last changes fastest.
Arguments:
- returns: bfloat16 [256, 2097152], P(None, 'span'), may hold values from -40 to 40
- market: bfloat16 [2097152], P('span'), may hold values from -12 to 12
- mask: int32 [2097152], P('span'), may hold values 0 or 1
- counts: int32 [256], P('span'), may hold values from 0 to 8192, as said below
Outputs:
- slope: float32 [256, 1048576], P(None, 'span')
Inputs may be any that keep to these rules, and one draw needn't show every extreme that they name: For every span d, the counts of spans 0 to d sum to between (d + 1) * 4096 and (d + 2) * 4096; all counts sum to exactly 1048576; some span holds exactly 8192.
All inputs are finite; a program needn't handle non-finite values. No bound on the sum of `mask` on one device may be relied on, other than what follows from the above.
Results may differ from a plain program's by a relative error of at most 0.00039.
Values may be sent and summed in bfloat16 or wider, within the bound.
A program may use at most 64 MiB of HBM per device.

v0:
```python
import jax
import jax.numpy as jnp
from jax import lax
from jax.sharding import Mesh
from jax.sharding import PartitionSpec as P

WIN = 1024
BLOCK = 512
QROWS = 4096
SPAN = ("span_0", "span_1", "span_2", "span_3")
RIDGE = 0.1


def in_order(parts, dim):
    parts = jnp.moveaxis(parts, 0, dim)
    dims = parts.shape
    return parts.reshape(*dims[:dim], dims[dim] * dims[dim + 1], *dims[dim + 2 :])


def stacked_from(x, axes, sequence):
    parts = x[None]
    for k in sequence:
        parts = lax.all_gather(parts, axes[k], axis=0, tiled=True)
    block = [lax.axis_size(axes[k]) for k in reversed(sequence)]
    parts = parts.reshape(*block, *x.shape)
    turned = sorted(range(len(sequence)), key=lambda place: sequence[len(sequence) - 1 - place])
    return parts.transpose(*turned, *range(len(sequence), parts.ndim)).reshape(-1, *x.shape)


def whole_of(x, axes, sequence, dim):
    return in_order(stacked_from(x, axes, sequence), dim)


def shifted(value, axis, steps):
    count = lax.axis_size(axis)
    initial, last = (max(0, -steps), min(count, count - steps))
    return lax.ppermute(value, axis, [(source, source + steps) for source in range(initial, last)])


def band_matrix():
    row_index = jnp.arange(BLOCK + WIN, dtype=jnp.int32)[:, None]
    col_index = jnp.arange(BLOCK, dtype=jnp.int32)[None, :]
    inside = (row_index >= col_index + 1) & (row_index <= col_index + WIN)
    return inside.astype(jnp.bfloat16)


def stacked(y_values, x_values, w_values):
    cross_terms = (x_values.astype(jnp.float32)[None, :] * y_values.astype(jnp.float32)).astype(
        jnp.bfloat16
    )
    square = (x_values.astype(jnp.float32) * x_values.astype(jnp.float32)).astype(jnp.bfloat16)
    return jnp.concatenate(
        [cross_terms, y_values, w_values[None, :], x_values[None, :], square[None, :]], 0
    )


def slopes_of(moments):
    stocks = (moments.shape[0] - 3) // 2
    sum_xy = moments[:stocks]
    sum_y = moments[stocks : 2 * stocks]
    sum_w = moments[2 * stocks]
    sum_x = moments[2 * stocks + 1]
    sum_xx = moments[2 * stocks + 2]
    numerator = sum_w * sum_xy - sum_x * sum_y
    denominator = sum_w * sum_xx - sum_x * sum_x + RIDGE * WIN * WIN
    return numerator / denominator


def per_device(returns, market, mask, counts):
    quota = QROWS
    my_index = lax.axis_index(SPAN)
    own_count = counts[0]
    gathered = whole_of(counts, (("span_0", "span_1", "span_2"), "span_3"), (0, 1), 0)
    earlier = jnp.arange(gathered.shape[0], dtype=jnp.int32) < my_index
    before = jnp.sum(jnp.where(earlier, gathered, 0))
    capacity = returns.shape[1]
    row_index = jnp.arange(capacity, dtype=jnp.int32)
    weight = jnp.where(row_index < own_count, mask, 0).astype(jnp.float32)
    y_values = (returns.astype(jnp.float32) * weight[None, :]).astype(jnp.bfloat16)
    x_values = (market.astype(jnp.float32) * weight).astype(jnp.bfloat16)
    combined = jnp.concatenate(
        [y_values, x_values[None, :], weight.astype(jnp.bfloat16)[None, :]], 0
    )
    padded = jnp.pad(combined, ((0, 0), (quota, 0)))
    shift_base = my_index * quota - before

    def take_rows(first, length):
        return lax.dynamic_slice_in_dim(padded, first + quota, length, 1)

    own_rows = take_rows(shift_base, quota)
    near_piece = shifted(take_rows(shift_base + quota - WIN, quota + WIN), SPAN, 1)
    far_piece = shifted(take_rows(shift_base + 2 * quota - WIN, WIN), SPAN, 2)
    halo_rows = near_piece[:, :WIN] + far_piece
    window = own_rows + near_piece[:, WIN:]
    extended = jnp.concatenate([halo_rows, window], 1)
    stocks = extended.shape[0] - 2
    stacked_rows = stacked(extended[:stocks], extended[stocks], extended[stocks + 1])
    band_ones = band_matrix()

    def one_block(block_index):
        window_piece = lax.dynamic_slice_in_dim(stacked_rows, block_index * BLOCK, BLOCK + WIN, 1)
        return slopes_of(jnp.dot(window_piece, band_ones, preferred_element_type=jnp.float32))

    blocks = lax.map(one_block, jnp.arange(quota // BLOCK, dtype=jnp.int32))
    return jnp.transpose(blocks, (1, 0, 2)).reshape(stocks, quota)


def solution(mesh):
    finer = Mesh(mesh.devices.reshape(4, 4, 8, 2), ("span_0", "span_1", "span_2", "span_3"))
    return jax.shard_map(
        per_device,
        mesh=finer,
        in_specs=(P(None, SPAN), P(SPAN), P(SPAN), P(SPAN)),
        out_specs=P(None, SPAN),
        check_vma=False,
    )
```

profile of v0, /device:TPU:9, one launch (start us, length us, event | category | flops | bytes accessed | tf_op | source)
XLA Modules:
  0.0 168.3 jit_solution(13319208394564157042)
XLA Ops:
  0.7 1.3 dynamic-slice
  2.7 23.9 %all-reduce.1 = s32[128]{0:T(128)S(1)} all-reduce(s32[128]{0:T(128)S(1)} %dynamic-update-slice), channel_id=2, replica_groups=mesh['span_0'=4,'span_1'=4,'span_2'=8,'span_3'=2] {'span_0','span_1','sp..., use_global_device_ids=true, to_apply=%add.1 | all-reduce | flops 128 | bytes 1024
  26.6 8.1 %all-gather.2 = s32[2,1,128]{2,1,0:T(1,128)S(1)} all-gather(s32[1,1,128]{2,1,0:T(1,128)S(1)} %bitcast.34), channel_id=3, replica_groups=mesh['span_0'=4,'span_1'=4,'span_2'=8,'span_3'=2] {'span_3'}, dimensions={0}, use_global_device_ids=true | all-gather | bytes 1536 | tf_op jit(solution)/shard_map/all_gather | solution.py:23
  36.7 5.2 %multiply_convert_fusion = bf16[256,8192]{1,0:T(8,128)(2,1)} fusion(bf16[256,8192]{1,0:T(8,128)(2,1)} %param.6, f32[8192]{0:T(1024)S(1)} %get-tuple-element.66), kind=kLoop, calls=%fused_computation.23 | loop fusion | flops 6291456 | bytes 8421376 | tf_op jit(solution)/shard_map/convert_element_type | solution.py:79
  41.9 3.9 %fusion.20 = bf16[258,12288]{1,0:T(8,128)(2,1)S(1)} fusion(bf16[1,8192]{1,0:T(2,128)(2,1)S(1)} %broadcast_in_dim.33, bf16[1,8192]{1,0:T(2,128)(2,1)S(1)} %broadcast_in_dim.32, bf16[256,8192]{1,0:T(8,128)(2,1)} %multiply_convert_fusion), kind=kLoop, calls=%fused_computation.25 | loop fusion | flops 31703040 | bytes 10567680 | tf_op jit(solution)/shard_map/concatenate | solution.py:81
  45.8 2.7 %copy-done = bf16[258,12288]{1,0:T(8,128)(2,1)} copy-done((bf16[258,12288]{1,0:T(8,128)(2,1)}, bf16[258,12288]{1,0:T(8,128)(2,1)S(1)}, u32[]{:S(2)}) %copy-start) | copy-done | bytes 6340632
  48.5 2.6 %constant_dynamic-slice_fusion.1 = bf16[258,5120]{1,0:T(8,128)(2,1)} fusion(bf16[258,12288]{1,0:T(8,128)(2,1)S(1)} %fusion.20, s32[]{:T(128)S(6)} %select_n.23), kind=kLoop, calls=%fused_computation.43 | loop fusion | bytes 5283844 | tf_op jit(solution)/shard_map/dynamic_slice | solution.py:88
  51.1 2.9 %collective-permute-start = (bf16[258,5120]{1,0:T(8,128)(2,1)}, bf16[258,5120]{1,0:T(8,128)(2,1)S(1)}, u32[]{:S(2)}, u32[]{:S(2)}) collective-permute-start(bf16[258,5120]{1,0:T(8,128)(2,1)} %constant_dynamic-slice_fusion.1), channel_id=1, source_target_pairs={{0,1},{1,2},{2,3},{3,4},{4,5},{5,6},{6,7},{7,8},{8,9},{9,10},{10,1... | collective-permute-start | bytes 7925768 | tf_op jit(solution)/shard_map/ppermute | solution.py:37
  54.0 2.1 %constant_dynamic-slice_fusion = bf16[258,1024]{1,0:T(8,128)(2,1)} fusion(bf16[258,12288]{1,0:T(8,128)(2,1)} %copy-done, s32[]{:T(128)S(6)} %select_n.24), kind=kLoop, calls=%fused_computation.42 | loop fusion | bytes 1056772 | tf_op jit(solution)/shard_map/dynamic_slice | solution.py:88
  56.1 2.6 %collective-permute-start.1 = (bf16[258,1024]{1,0:T(8,128)(2,1)}, bf16[258,1024]{1,0:T(8,128)(2,1)S(1)}, u32[]{:S(2)}, u32[]{:S(2)}) collective-permute-start(bf16[258,1024]{1,0:T(8,128)(2,1)} %constant_dynamic-slice_fusion), channel_id=1, source_target_pairs={{0,2},{1,3},{2,4},{3,5},{4,6},{5,7},{6,8},{7,9},{8,10},{9,11},{10,... | collective-permute-start | bytes 1585160 | tf_op jit(solution)/shard_map/ppermute | solution.py:37
  58.8 41.9 %collective-permute-done.1 = bf16[258,1024]{1,0:T(8,128)(2,1)S(1)} collective-permute-done((bf16[258,1024]{1,0:T(8,128)(2,1)}, bf16[258,1024]{1,0:T(8,128)(2,1)S(1)}, u32[]{:S(2)}, u32[]{:S(2)}) %collective-permute-start.1) | collective-permute-done | bytes 528416 | tf_op jit(solution)/shard_map/ppermute | solution.py:37
  100.7 2.8 %slice_add_fusion = bf16[258,4096]{1,0:T(8,128)(2,1)S(1)} fusion(bf16[258,5120]{1,0:T(8,128)(2,1)S(1)} %collective-permute-done, bf16[258,12288]{1,0:T(8,128)(2,1)} %copy-done, s32[]{:T(128)S(6)} %select_n.25), kind=kLoop, calls=%fused_computation.30 | loop fusion | flops 4227072 | bytes 6340612 | tf_op jit(solution)/shard_map/add | solution.py:94
  103.7 2.0 %multiply_convert_fusion.1 = (bf16[256,5120]{1,0:T(8,128)(2,1)S(1)}, bf16[256,5120]{1,0:T(8,128)(2,1)}) fusion(f32[5120]{0:T(1024)S(1)} %bitcast.32, bf16[258,4096]{1,0:T(8,128)(2,1)S(1)} %slice_add_fusion, bf16[258,1024]{1,0:T(8,128)(2,1)S(1)} %slice_add_fusion.1), kind=kLoop, calls=%fused_computation.26 | loop fusion | flops 9175040 | bytes 7905280 | tf_op jit(solution)/shard_map/convert_element_type | solution.py:48
  105.7 19.2 %concatenate.11 = bf16[515,5120]{1,0:T(8,128)(2,1)} concatenate(bf16[256,5120]{1,0:T(8,128)(2,1)S(1)} %get-tuple-element.63, bf16[256,5120]{1,0:T(8,128)(2,1)} %get-tuple-element.64, bf16[1,5120]{1,0:T(2,128)(2,1)S(1)} %pad_maximum_fusion, bf16[1,5120]{1,0:T(2,128)(2,1)S(1)} %get-tuple-element.62, bf16[1,5120]{1,0:T(2,128)(2,1)S(1)} %get-tuple-element.61), dimensions={0} | concatenate | bytes 10547200 | tf_op jit(solution)/shard_map/concatenate | solution.py:52
  124.9 38.6 %while.11 = (s32[]{:T(128)}, f32[8,256,512]{2,1,0:T(8,128)}, s32[8]{0:T(128)S(1)}, bf16[515,5120]{1,0:T(8,128)(2,1)}, s32[512]{0:T(512)S(1)}, /*index=5*/s32[512...) while((s32[]{:T(128)}, f32[8,256,512]{2,1,0:T(8,128)}, s32[8]{0:T(128)S(1)}, ...), condition=%wide.region_2.3_spmd.clone, body=%wide.region_1.2_spmd.clone.sunk | while | flops 813697024 | bytes 4248227 | solution.py:104
  126.1 2.6 %fusion.32 = f32[515,512]{1,0:T(8,128)S(1)} fusion(bf16[515,5120]{1,0:T(8,128)(2,1)} %get-tuple-element.138, s32[]{:T(128)S(6)} %select_n.33, s32[512]{0:T(512)S(1)} %get-tuple-element.140, s32[512]{0:T(512)S(1)} %get-tuple-element.139), kind=kOutput, calls=%fused_computation.5.clone.1 | convolution fusion | flops 813170688 | bytes 2656260 | tf_op jit(solution)/shard_map/while/body/eval_jaxpr/dot_general | solution.py:102
  128.8 0.9 fusion.34
  131.0 2.6 %fusion.32 = f32[515,512]{1,0:T(8,128)S(1)} fusion(bf16[515,5120]{1,0:T(8,128)(2,1)} %get-tuple-element.138, s32[]{:T(128)S(6)} %select_n.33, s32[512]{0:T(512)S(1)} %get-tuple-element.140, s32[512]{0:T(512)S(1)} %get-tuple-element.139), kind=kOutput, calls=%fused_computation.5.clone.1 | convolution fusion | flops 813170688 | bytes 2656260 | tf_op jit(solution)/shard_map/while/body/eval_jaxpr/dot_general | solution.py:102
  133.6 0.9 fusion.34
  135.8 2.6 %fusion.32 = f32[515,512]{1,0:T(8,128)S(1)} fusion(bf16[515,5120]{1,0:T(8,128)(2,1)} %get-tuple-element.138, s32[]{:T(128)S(6)} %select_n.33, s32[512]{0:T(512)S(1)} %get-tuple-element.140, s32[512]{0:T(512)S(1)} %get-tuple-element.139), kind=kOutput, calls=%fused_computation.5.clone.1 | convolution fusion | flops 813170688 | bytes 2656260 | tf_op jit(solution)/shard_map/while/body/eval_jaxpr/dot_general | solution.py:102
  138.4 0.9 fusion.34
  140.6 2.6 %fusion.32 = f32[515,512]{1,0:T(8,128)S(1)} fusion(bf16[515,5120]{1,0:T(8,128)(2,1)} %get-tuple-element.138, s32[]{:T(128)S(6)} %select_n.33, s32[512]{0:T(512)S(1)} %get-tuple-element.140, s32[512]{0:T(512)S(1)} %get-tuple-element.139), kind=kOutput, calls=%fused_computation.5.clone.1 | convolution fusion | flops 813170688 | bytes 2656260 | tf_op jit(solution)/shard_map/while/body/eval_jaxpr/dot_general | solution.py:102
  143.2 1.0 fusion.34
  145.4 2.6 %fusion.32 = f32[515,512]{1,0:T(8,128)S(1)} fusion(bf16[515,5120]{1,0:T(8,128)(2,1)} %get-tuple-element.138, s32[]{:T(128)S(6)} %select_n.33, s32[512]{0:T(512)S(1)} %get-tuple-element.140, s32[512]{0:T(512)S(1)} %get-tuple-element.139), kind=kOutput, calls=%fused_computation.5.clone.1 | convolution fusion | flops 813170688 | bytes 2656260 | tf_op jit(solution)/shard_map/while/body/eval_jaxpr/dot_general | solution.py:102
  148.0 1.0 fusion.34
  150.2 2.6 %fusion.32 = f32[515,512]{1,0:T(8,128)S(1)} fusion(bf16[515,5120]{1,0:T(8,128)(2,1)} %get-tuple-element.138, s32[]{:T(128)S(6)} %select_n.33, s32[512]{0:T(512)S(1)} %get-tuple-element.140, s32[512]{0:T(512)S(1)} %get-tuple-element.139), kind=kOutput, calls=%fused_computation.5.clone.1 | convolution fusion | flops 813170688 | bytes 2656260 | tf_op jit(solution)/shard_map/while/body/eval_jaxpr/dot_general | solution.py:102
  152.9 0.9 fusion.34
  155.1 2.6 %fusion.32 = f32[515,512]{1,0:T(8,128)S(1)} fusion(bf16[515,5120]{1,0:T(8,128)(2,1)} %get-tuple-element.138, s32[]{:T(128)S(6)} %select_n.33, s32[512]{0:T(512)S(1)} %get-tuple-element.140, s32[512]{0:T(512)S(1)} %get-tuple-element.139), kind=kOutput, calls=%fused_computation.5.clone.1 | convolution fusion | flops 813170688 | bytes 2656260 | tf_op jit(solution)/shard_map/while/body/eval_jaxpr/dot_general | solution.py:102
  157.7 0.9 fusion.34
  159.9 2.6 %fusion.32 = f32[515,512]{1,0:T(8,128)S(1)} fusion(bf16[515,5120]{1,0:T(8,128)(2,1)} %get-tuple-element.138, s32[]{:T(128)S(6)} %select_n.33, s32[512]{0:T(512)S(1)} %get-tuple-element.140, s32[512]{0:T(512)S(1)} %get-tuple-element.139), kind=kOutput, calls=%fused_computation.5.clone.1 | convolution fusion | flops 813170688 | bytes 2656260 | tf_op jit(solution)/shard_map/while/body/eval_jaxpr/dot_general | solution.py:102
  162.5 0.9 fusion.34
  163.5 4.8 %copy.7 = f32[8,32,8,512]{3,2,0,1:T(8,128)} copy(f32[8,32,8,512]{3,2,1,0:T(8,128)} %bitcast.13) | data formatting | bytes 8388608 | tf_op jit(solution)/shard_map/reshape | solution.py:105
  (32 shorter events, 7.1 us)
Async XLA Ops:
  45.8 2.7 %copy-start = (bf16[258,12288]{1,0:T(8,128)(2,1)}, bf16[258,12288]{1,0:T(8,128)(2,1)S(1)}, u32[]{:S(2)}) copy-start(bf16[258,12288]{1,0:T(8,128)(2,1)S(1)} %fusion.20) | copy-start | bytes 19021828
  51.1 49.5 %collective-permute-start = (bf16[258,5120]{1,0:T(8,128)(2,1)}, bf16[258,5120]{1,0:T(8,128)(2,1)S(1)}, u32[]{:S(2)}, u32[]{:S(2)}) collective-permute-start(bf16[258,5120]{1,0:T(8,128)(2,1)} %constant_dynamic-slice_fusion.1), channel_id=1, source_target_pairs={{0,1},{1,2},{2,3},{3,4},{4,5},{5,6},{6,7},{7,8},{8,9},{9,10},{10,1... | collective-permute-start | bytes 7925768 | tf_op jit(solution)/shard_map/ppermute | solution.py:37
  56.1 44.5 %collective-permute-start.1 = (bf16[258,1024]{1,0:T(8,128)(2,1)}, bf16[258,1024]{1,0:T(8,128)(2,1)S(1)}, u32[]{:S(2)}, u32[]{:S(2)}) collective-permute-start(bf16[258,1024]{1,0:T(8,128)(2,1)} %constant_dynamic-slice_fusion), channel_id=1, source_target_pairs={{0,2},{1,3},{2,4},{3,5},{4,6},{5,7},{6,8},{7,9},{8,10},{9,11},{10,... | collective-permute-start | bytes 1585160 | tf_op jit(solution)/shard_map/ppermute | solution.py:37
where the time goes:
time: 169 us; the launch traced here: 168 us
  waiting for transfers between devices  41.9 us (25%)
  local copies, waits for them, and re-layouts  38.2 us (23%)
  blocking collectives  31.9 us (19%)
  other arithmetic  23.1 us (14%)
  matrix products  21 us (12%)
  starting transfers between devices  5.48 us (3%)
  loops' own time  5.37 us (3%)
    ppermute x2, waiting for transfers between devices, shifted(): lax.ppermute(value, axis, [(source, source + steps) for source in range(i...  41.9 us
    unnamed x1, blocking collectives  23.9 us
    dot_general x8, matrix products, one_block(): jnp.dot(window_piece, band_ones, preferred_element_type=jnp.float32)  21 us
    concatenate x1, local copies, waits for them, and re-layouts, stacked(): jnp.concatenate([cross_terms, y_values, w_values[None, :], x_values[None,...  19.2 us
    all_gather x1, blocking collectives, stacked_from(): parts = lax.all_gather(parts, axes[k], axis=0, tiled=True)  8.07 us
    dynamic_update_slice x8, other arithmetic, per_device(): blocks = lax.map(one_block, jnp.arange(quota // BLOCK, dtype=jnp.int32))  7.47 us
    ppermute x2, starting transfers between devices, shifted(): lax.ppermute(value, axis, [(source, source + steps) for source in range(i...  5.48 us
    another operation x1, loops' own time, per_device(): blocks = lax.map(one_block, jnp.arange(quota // BLOCK, dtype=jnp.int32))  5.37 us
  transfers between devices with their start and end apart: 2, of which 1 were waited for; matrix products, arithmetic and copies ran while one was open for 1% of the time, Pallas kernels for 0%

commit v1 on v0

--- a/solution.py
+++ b/solution.py
@@ -20,7 +20,8 @@
 def stacked_from(x, axes, sequence):
     parts = x[None]
     for k in sequence:
-        parts = lax.all_gather(parts, axes[k], axis=0, tiled=True)
+        outgoing = jnp.stack([parts] * lax.axis_size(axes[k]))
+        parts = jnp.concatenate(lax.all_to_all(outgoing, axes[k], 0, 0), axis=0)
     block = [lax.axis_size(axes[k]) for k in reversed(sequence)]
     parts = parts.reshape(*block, *x.shape)
     turned = sorted(range(len(sequence)), key=lambda place: sequence[len(sequence) - 1 - place])

time: 169 us -> 158 us (0.935)
  blocking collectives: 31.9 us -> 5.46 us
  starting transfers between devices: 5.48 us -> 19.7 us
  local copies, waits for them, and re-layouts: 38.2 us -> 35.9 us
    unnamed x1 -> x0, blocking collectives: 23.9 us -> none
    all_to_all x0 -> x1, starting transfers between devices: none -> 14.9 us  [stacked_from(): parts = jnp.concatenate(lax.all_to_all(outgoing, axes[k], 0, 0), axis=0)]
    all_gather x1 -> x0, blocking collectives: 8.07 us -> none  [stacked_from(): parts = lax.all_gather(parts, axes[k], axis=0, tiled=True)]
    all_to_all x0 -> x1, blocking collectives: none -> 5.46 us  [stacked_from(): parts = jnp.concatenate(lax.all_to_all(outgoing, axes[k], 0, 0), axis=0)]
    unnamed x5 -> x0, local copies, waits for them, and re-layouts: 4.72 us -> none
    all_to_all x0 -> x1, other arithmetic: none -> 2.35 us  [stacked_from(): parts = jnp.concatenate(lax.all_to_all(outgoing, axes[k], 0, 0), axis=0)]
    convert_element_type x1, other arithmetic: 5.16 us -> 3.35 us  [per_device(): (returns.astype(jnp.float32) * weight[None, :]).astype(jnp.bfloat16)]
    dynamic_slice x2, local copies, waits for them, and re-layouts: 4.72 us -> 6.48 us  [take_rows(): return lax.dynamic_slice_in_dim(padded, first + quota, length, 1)]
  transfers between devices with their start and end apart: 2 -> 3, of which waited for: 1 -> 2; matrix products, arithmetic and copies ran while one was open for 1% -> 7% of each run, Pallas kernels for 0% -> 0%
where the time goes in v1:
time: 158 us; the launch traced here: 157 us
  waiting for transfers between devices  43.3 us (27%)
  local copies, waits for them, and re-layouts  35.9 us (23%)
  other arithmetic  24.7 us (16%)
  matrix products  21 us (13%)
  starting transfers between devices  19.7 us (12%)
  blocking collectives  5.46 us (3%)
  loops' own time  5.37 us (3%)
    ppermute x2, waiting for transfers between devices, shifted(): lax.ppermute(value, axis, [(source, source + steps) for source in range(i...  42.5 us
    dot_general x8, matrix products, one_block(): jnp.dot(window_piece, band_ones, preferred_element_type=jnp.float32)  21 us
    concatenate x1, local copies, waits for them, and re-layouts, stacked(): jnp.concatenate([cross_terms, y_values, w_values[None, :], x_values[None,...  19.2 us
    all_to_all x1, starting transfers between devices, stacked_from(): parts = jnp.concatenate(lax.all_to_all(outgoing, axes[k], 0, 0), axis=0)  14.9 us
    dynamic_update_slice x8, other arithmetic, per_device(): blocks = lax.map(one_block, jnp.arange(quota // BLOCK, dtype=jnp.int32))  7.51 us
    dynamic_slice x2, local copies, waits for them, and re-layouts, take_rows(): return lax.dynamic_slice_in_dim(padded, first + quota, length, 1)  6.48 us
    all_to_all x1, blocking collectives, stacked_from(): parts = jnp.concatenate(lax.all_to_all(outgoing, axes[k], 0, 0), axis=0)  5.46 us
    another operation x1, loops' own time, per_device(): blocks = lax.map(one_block, jnp.arange(quota // BLOCK, dtype=jnp.int32))  5.37 us
  transfers between devices with their start and end apart: 3, of which 2 were waited for; matrix products, arithmetic and copies ran while one was open for 7% of the time, Pallas kernels for 0%

profile of v1, /device:TPU:9, one launch (start us, length us, event | category | flops | bytes accessed | tf_op | source)
XLA Modules:
  0.0 156.8 jit_solution(16957464072776374625)
XLA Ops:
  1.3 14.9 %all-to-all-start = ((s32[128,1,1]{2,1,0:T(1,128)}), s32[128,1,1]{2,1,0:T(1,128)S(1)}, u32[]{:S(2)}, u32[]{:S(2)}) async-start(s32[128,1,1]{2,1,0:T(1,128)} %stack.6), calls=%async_computation | async-start | bytes 131072 | tf_op jit(solution)/shard_map/all_to_all | solution.py:24
  16.2 0.8 multiply_convert_fusion.2
  17.0 3.3 %multiply_convert_fusion = bf16[256,8192]{1,0:T(8,128)(2,1)S(1)} fusion(bf16[256,8192]{1,0:T(8,128)(2,1)} %param.6, f32[8192]{0:T(1024)S(1)} %get-tuple-element.66), kind=kLoop, calls=%fused_computation.23 | loop fusion | flops 6291456 | bytes 8421376 | tf_op jit(solution)/shard_map/convert_element_type | solution.py:80
  20.4 5.0 %fusion.20 = bf16[258,12288]{1,0:T(8,128)(2,1)} fusion(bf16[1,8192]{1,0:T(2,128)(2,1)S(1)} %broadcast_in_dim.30, bf16[1,8192]{1,0:T(2,128)(2,1)S(1)} %broadcast_in_dim.29, bf16[256,8192]{1,0:T(8,128)(2,1)S(1)} %multiply_convert_fusion), kind=kLoop, calls=%fused_computation.25 | loop fusion | flops 31703040 | bytes 10567680 | tf_op jit(solution)/shard_map/concatenate | solution.py:82
  26.1 2.3 %reduce.1 = s32[128]{0:T(128)S(1)} reduce(s32[128,1,1]{2,1,0:T(1,128)S(1)} %all-to-all-done, s32[]{:T(128)} %constant.52.clone.1), dimensions={1,2}, to_apply=%all_to_all.6.reduce_sub_computation | reduce | bytes 1028 | tf_op jit(solution)/shard_map/all_to_all | solution.py:24
  28.5 5.5 %all_to_all.10 = s32[2,128,1]{1,2,0:T(1,128)S(1)} all-to-all(s32[2,128,1]{1,2,0:T(1,128)S(1)} %pad_add_fusion), channel_id=1, replica_groups=mesh['span_0'=4,'span_1'=4,'span_2'=8,'span_3'=2] {'span_3'}, dimensions={0} | all-to-all | bytes 2048 | tf_op jit(solution)/shard_map/all_to_all | solution.py:24
  35.3 4.4 %constant_dynamic-slice_fusion.1 = bf16[258,5120]{1,0:T(8,128)(2,1)} fusion(bf16[258,12288]{1,0:T(8,128)(2,1)} %fusion.20, s32[]{:T(128)S(6)} %select_n.23), kind=kLoop, calls=%fused_computation.44 | loop fusion | bytes 5283844 | tf_op jit(solution)/shard_map/dynamic_slice | solution.py:89
  39.6 2.5 %collective-permute-start = (bf16[258,5120]{1,0:T(8,128)(2,1)}, bf16[258,5120]{1,0:T(8,128)(2,1)S(1)}, u32[]{:S(2)}, u32[]{:S(2)}) collective-permute-start(bf16[258,5120]{1,0:T(8,128)(2,1)} %constant_dynamic-slice_fusion.1), channel_id=1, source_target_pairs={{0,1},{1,2},{2,3},{3,4},{4,5},{5,6},{6,7},{7,8},{8,9},{9,10},{10,1... | collective-permute-start | bytes 7925768 | tf_op jit(solution)/shard_map/ppermute | solution.py:38
  42.1 2.1 %constant_dynamic-slice_fusion = bf16[258,1024]{1,0:T(8,128)(2,1)} fusion(bf16[258,12288]{1,0:T(8,128)(2,1)} %fusion.20, s32[]{:T(128)S(6)} %select_n.24), kind=kLoop, calls=%fused_computation.43 | loop fusion | bytes 1056772 | tf_op jit(solution)/shard_map/dynamic_slice | solution.py:89
  44.2 2.3 %collective-permute-start.1 = (bf16[258,1024]{1,0:T(8,128)(2,1)}, bf16[258,1024]{1,0:T(8,128)(2,1)S(1)}, u32[]{:S(2)}, u32[]{:S(2)}) collective-permute-start(bf16[258,1024]{1,0:T(8,128)(2,1)} %constant_dynamic-slice_fusion), channel_id=1, source_target_pairs={{0,2},{1,3},{2,4},{3,5},{4,6},{5,7},{6,8},{7,9},{8,10},{9,11},{10,... | collective-permute-start | bytes 1585160 | tf_op jit(solution)/shard_map/ppermute | solution.py:38
  46.6 42.5 %collective-permute-done.1 = bf16[258,1024]{1,0:T(8,128)(2,1)S(1)} collective-permute-done((bf16[258,1024]{1,0:T(8,128)(2,1)}, bf16[258,1024]{1,0:T(8,128)(2,1)S(1)}, u32[]{:S(2)}, u32[]{:S(2)}) %collective-permute-start.1) | collective-permute-done | bytes 528416 | tf_op jit(solution)/shard_map/ppermute | solution.py:38
  89.2 2.8 %slice_add_fusion = bf16[258,4096]{1,0:T(8,128)(2,1)S(1)} fusion(bf16[258,5120]{1,0:T(8,128)(2,1)S(1)} %collective-permute-done, bf16[258,12288]{1,0:T(8,128)(2,1)} %fusion.20, s32[]{:T(128)S(6)} %select_n.25), kind=kLoop, calls=%fused_computation.30 | loop fusion | flops 4227072 | bytes 6340612 | tf_op jit(solution)/shard_map/add | solution.py:95
  92.1 2.0 %multiply_convert_fusion.1 = (bf16[256,5120]{1,0:T(8,128)(2,1)S(1)}, bf16[256,5120]{1,0:T(8,128)(2,1)}) fusion(f32[5120]{0:T(1024)S(1)} %bitcast.33, bf16[258,4096]{1,0:T(8,128)(2,1)S(1)} %slice_add_fusion, bf16[258,1024]{1,0:T(8,128)(2,1)S(1)} %slice_add_fusion.1), kind=kLoop, calls=%fused_computation.26 | loop fusion | flops 9175040 | bytes 7905280 | tf_op jit(solution)/shard_map/convert_element_type | solution.py:49
  94.2 19.2 %concatenate.11 = bf16[515,5120]{1,0:T(8,128)(2,1)} concatenate(bf16[256,5120]{1,0:T(8,128)(2,1)S(1)} %get-tuple-element.63, bf16[256,5120]{1,0:T(8,128)(2,1)} %get-tuple-element.64, bf16[1,5120]{1,0:T(2,128)(2,1)S(1)} %pad_maximum_fusion, bf16[1,5120]{1,0:T(2,128)(2,1)S(1)} %get-tuple-element.62, bf16[1,5120]{1,0:T(2,128)(2,1)S(1)} %get-tuple-element.61), dimensions={0} | concatenate | bytes 10547200 | tf_op jit(solution)/shard_map/concatenate | solution.py:53
  113.4 38.6 %while.11 = (s32[]{:T(128)}, f32[8,256,512]{2,1,0:T(8,128)}, s32[8]{0:T(128)S(1)}, bf16[515,5120]{1,0:T(8,128)(2,1)}, s32[512]{0:T(512)S(1)}, /*index=5*/s32[512...) while((s32[]{:T(128)}, f32[8,256,512]{2,1,0:T(8,128)}, s32[8]{0:T(128)S(1)}, ...), condition=%wide.region_2.3_spmd.clone, body=%wide.region_1.2_spmd.clone.sunk | while | flops 813697024 | bytes 4248227 | solution.py:105
  114.6 2.6 %fusion.32 = f32[515,512]{1,0:T(8,128)S(1)} fusion(bf16[515,5120]{1,0:T(8,128)(2,1)} %get-tuple-element.138, s32[]{:T(128)S(6)} %select_n.33, s32[512]{0:T(512)S(1)} %get-tuple-element.140, s32[512]{0:T(512)S(1)} %get-tuple-element.139), kind=kOutput, calls=%fused_computation.5.clone.1 | convolution fusion | flops 813170688 | bytes 2656260 | tf_op jit(solution)/shard_map/while/body/eval_jaxpr/dot_general | solution.py:103
  117.2 0.9 fusion.34
  119.4 2.6 %fusion.32 = f32[515,512]{1,0:T(8,128)S(1)} fusion(bf16[515,5120]{1,0:T(8,128)(2,1)} %get-tuple-element.138, s32[]{:T(128)S(6)} %select_n.33, s32[512]{0:T(512)S(1)} %get-tuple-element.140, s32[512]{0:T(512)S(1)} %get-tuple-element.139), kind=kOutput, calls=%fused_computation.5.clone.1 | convolution fusion | flops 813170688 | bytes 2656260 | tf_op jit(solution)/shard_map/while/body/eval_jaxpr/dot_general | solution.py:103
  122.1 0.9 fusion.34
  124.2 2.6 %fusion.32 = f32[515,512]{1,0:T(8,128)S(1)} fusion(bf16[515,5120]{1,0:T(8,128)(2,1)} %get-tuple-element.138, s32[]{:T(128)S(6)} %select_n.33, s32[512]{0:T(512)S(1)} %get-tuple-element.140, s32[512]{0:T(512)S(1)} %get-tuple-element.139), kind=kOutput, calls=%fused_computation.5.clone.1 | convolution fusion | flops 813170688 | bytes 2656260 | tf_op jit(solution)/shard_map/while/body/eval_jaxpr/dot_general | solution.py:103
  126.8 0.9 fusion.34
  129.0 2.6 %fusion.32 = f32[515,512]{1,0:T(8,128)S(1)} fusion(bf16[515,5120]{1,0:T(8,128)(2,1)} %get-tuple-element.138, s32[]{:T(128)S(6)} %select_n.33, s32[512]{0:T(512)S(1)} %get-tuple-element.140, s32[512]{0:T(512)S(1)} %get-tuple-element.139), kind=kOutput, calls=%fused_computation.5.clone.1 | convolution fusion | flops 813170688 | bytes 2656260 | tf_op jit(solution)/shard_map/while/body/eval_jaxpr/dot_general | solution.py:103
  131.7 1.0 fusion.34
  133.9 2.6 %fusion.32 = f32[515,512]{1,0:T(8,128)S(1)} fusion(bf16[515,5120]{1,0:T(8,128)(2,1)} %get-tuple-element.138, s32[]{:T(128)S(6)} %select_n.33, s32[512]{0:T(512)S(1)} %get-tuple-element.140, s32[512]{0:T(512)S(1)} %get-tuple-element.139), kind=kOutput, calls=%fused_computation.5.clone.1 | convolution fusion | flops 813170688 | bytes 2656260 | tf_op jit(solution)/shard_map/while/body/eval_jaxpr/dot_general | solution.py:103
  136.5 1.0 fusion.34
  138.7 2.6 %fusion.32 = f32[515,512]{1,0:T(8,128)S(1)} fusion(bf16[515,5120]{1,0:T(8,128)(2,1)} %get-tuple-element.138, s32[]{:T(128)S(6)} %select_n.33, s32[512]{0:T(512)S(1)} %get-tuple-element.140, s32[512]{0:T(512)S(1)} %get-tuple-element.139), kind=kOutput, calls=%fused_computation.5.clone.1 | convolution fusion | flops 813170688 | bytes 2656260 | tf_op jit(solution)/shard_map/while/body/eval_jaxpr/dot_general | solution.py:103
  141.4 0.9 fusion.34
  143.5 2.6 %fusion.32 = f32[515,512]{1,0:T(8,128)S(1)} fusion(bf16[515,5120]{1,0:T(8,128)(2,1)} %get-tuple-element.138, s32[]{:T(128)S(6)} %select_n.33, s32[512]{0:T(512)S(1)} %get-tuple-element.140, s32[512]{0:T(512)S(1)} %get-tuple-element.139), kind=kOutput, calls=%fused_computation.5.clone.1 | convolution fusion | flops 813170688 | bytes 2656260 | tf_op jit(solution)/shard_map/while/body/eval_jaxpr/dot_general | solution.py:103
  146.2 0.9 fusion.34
  148.4 2.6 %fusion.32 = f32[515,512]{1,0:T(8,128)S(1)} fusion(bf16[515,5120]{1,0:T(8,128)(2,1)} %get-tuple-element.138, s32[]{:T(128)S(6)} %select_n.33, s32[512]{0:T(512)S(1)} %get-tuple-element.140, s32[512]{0:T(512)S(1)} %get-tuple-element.139), kind=kOutput, calls=%fused_computation.5.clone.1 | convolution fusion | flops 813170688 | bytes 2656260 | tf_op jit(solution)/shard_map/while/body/eval_jaxpr/dot_general | solution.py:103
  151.0 0.9 fusion.34
  151.9 4.8 %copy.8 = f32[8,32,8,512]{3,2,0,1:T(8,128)} copy(f32[8,32,8,512]{3,2,1,0:T(8,128)} %bitcast.10) | data formatting | bytes 8388608 | tf_op jit(solution)/shard_map/reshape | solution.py:106
  (31 shorter events, 7.0 us)
Async XLA Ops:
  1.3 24.8 %all-to-all-start = ((s32[128,1,1]{2,1,0:T(1,128)}), s32[128,1,1]{2,1,0:T(1,128)S(1)}, u32[]{:S(2)}, u32[]{:S(2)}) async-start(s32[128,1,1]{2,1,0:T(1,128)} %stack.6), calls=%async_computation | async-start | bytes 131072 | tf_op jit(solution)/shard_map/all_to_all | solution.py:24
  39.6 49.5 %collective-permute-start = (bf16[258,5120]{1,0:T(8,128)(2,1)}, bf16[258,5120]{1,0:T(8,128)(2,1)S(1)}, u32[]{:S(2)}, u32[]{:S(2)}) collective-permute-start(bf16[258,5120]{1,0:T(8,128)(2,1)} %constant_dynamic-slice_fusion.1), channel_id=1, source_target_pairs={{0,1},{1,2},{2,3},{3,4},{4,5},{5,6},{6,7},{7,8},{8,9},{9,10},{10,1... | collective-permute-start | bytes 7925768 | tf_op jit(solution)/shard_map/ppermute | solution.py:38
  44.2 44.9 %collective-permute-start.1 = (bf16[258,1024]{1,0:T(8,128)(2,1)}, bf16[258,1024]{1,0:T(8,128)(2,1)S(1)}, u32[]{:S(2)}, u32[]{:S(2)}) collective-permute-start(bf16[258,1024]{1,0:T(8,128)(2,1)} %constant_dynamic-slice_fusion), channel_id=1, source_target_pairs={{0,2},{1,3},{2,4},{3,5},{4,6},{5,7},{6,8},{7,9},{8,10},{9,11},{10,... | collective-permute-start | bytes 1585160 | tf_op jit(solution)/shard_map/ppermute | solution.py:38
